TPU v7x, 32 devices: a whole 2x2x4 slice. The times are simulated.
32 devices in a mesh: grp: 2 (over y), kvp: 4 (over z), tp: 4 (over x, core).
Axes of the slice: x: 2, y: 2, z: 4, core: 2. Of those that a mesh axis runs over, the one named last changes fastest.
Arguments:
- queries: bfloat16 [32, 4096], P('grp', 'tp'), parts along dimension 0, may hold values from -6 to 6
- keys: bfloat16 [32, 512, 512], P('grp', 'kvp', 'tp'), parts along dimension 0, may hold values from -6 to 6
- values: bfloat16 [32, 512, 512], P('grp', 'kvp', 'tp'), parts along dimension 0, may hold values from -6 to 6
- lengths: int32 [32], P('grp'), parts along dimension 0, may hold values from 256 to 512, as said below
- out_weight: bfloat16 [4096, 1536], P('tp', 'kvp'), may hold values from -0.375 to 0.375
- residual: bfloat16 [32, 1536], P('grp', 'kvp'), parts along dimension 0, may hold values from -20 to 20
- norm_gain: bfloat16 [1536], P('kvp'), may hold values from 0.099609375 to 1.8984375
- expert_ids: int32 [32, 4], P('grp'), parts along dimension 0, may hold values from 0 to 3, as said below
- gate_probs: float32 [32, 4], P('grp'), parts along dimension 0, may hold values from 0.2 to 1
- w_gate: bfloat16 [4, 1536, 1536], P('kvp', None, 'tp'), may hold values from -0.15625 to 0.15625
- w_up: bfloat16 [4, 1536, 1536], P('kvp', None, 'tp'), may hold values from -0.15625 to 0.15625
- w_down: bfloat16 [4, 1536, 1536], P('kvp', 'tp'), may hold values from -0.15625 to 0.15625
Outputs:
- attended: float32 [32, 4096], P('grp', 'tp'), parts along dimension 0
- mixed: bfloat16 [32, 1536], P('grp', 'kvp'), parts along dimension 0
There are 2 independent parts, one for each index of `grp`. A program takes and returns all parts, laid end to end along the dimension named above; an argument that names none is the same for every part. Nothing has to cross between parts.
Inputs may be any that keep to these rules, and one draw needn't show every extreme that they name: `lengths`: at least one sequence has all 512 positions valid. `expert_ids`: each row names 4 different experts; no expert is named by more than 16 rows, and some expert by exactly 16.
All inputs are finite; a program needn't handle non-finite values.
Results may differ from a plain program's by a relative error of at most 0.006.
Values may be sent and summed in bfloat16 or wider, within the bound.
No kernel may reach another device: no remote copies, remote signals or barrier semaphores. Data moves between devices by JAX's collectives and lax.ppermute only.
A program may use at most 64 MiB of HBM per device.

v0:
```python
import jax
import jax.numpy as jnp
from jax import lax
from jax.sharding import PartitionSpec as P

D = 1536
HEAD = 64
EPSILON = 1e-05
NEGATIVE = -1e30


def merged(part, axis, combine):
    gathered = jax.tree.map(lambda a: lax.all_gather(a, axis), part)

    def take(source):
        return jax.tree.map(lambda a: lax.dynamic_index_in_dim(a, source, 0, False), gathered)

    return lax.fori_loop(
        1, lax.axis_size(axis), lambda source, state: combine(state, take(source)), take(0)
    )


def slot_tables(expert_ids, gate_probs, experts, capacity):
    batch_size, top_count = expert_ids.shape
    flat_ids = expert_ids.reshape(-1)
    pair_count = flat_ids.shape[0]
    pair_order = jnp.arange(pair_count, dtype=jnp.int32)
    earlier_same = (flat_ids[:, None] == flat_ids[None, :]) & (
        pair_order[None, :] < pair_order[:, None]
    )
    slot_index = jnp.sum(earlier_same.astype(jnp.int32), axis=1)
    target_col = flat_ids * capacity + slot_index
    columns = jnp.arange(experts * capacity, dtype=jnp.int32)
    hit_table = (target_col[:, None] == columns[None, :]).astype(jnp.float32)
    hit_table = hit_table.reshape(batch_size, top_count, experts * capacity)
    dispatch = jnp.sum(hit_table, axis=1)
    combine = jnp.sum(hit_table * gate_probs[:, :, None], axis=1)
    return (dispatch, combine)


def merge_partial(earlier, latest):
    global_max = jnp.maximum(earlier[0], latest[0])
    lead_scale = jnp.exp(earlier[0] - global_max)
    trail_scale = jnp.exp(latest[0] - global_max)
    return (
        global_max,
        lead_scale * earlier[1] + trail_scale * latest[1],
        lead_scale[..., None] * earlier[2] + trail_scale[..., None] * latest[2],
    )


def on_device(
    queries,
    keys,
    values,
    lengths,
    out_weight,
    residual,
    norm_gain,
    expert_ids,
    gate_probs,
    w_gate,
    w_up,
    w_down,
):
    batch_size = queries.shape[0]
    local_kv = keys.shape[2] // HEAD
    local_heads = queries.shape[1] // HEAD
    group_size = local_heads // local_kv
    ctx_dev = keys.shape[1]
    shards = lax.axis_size("kvp")
    query_heads = queries.reshape(batch_size, local_kv, group_size, HEAD)
    key_rows = keys.reshape(batch_size, ctx_dev, local_kv, HEAD)
    value_rows = values.reshape(batch_size, ctx_dev, local_kv, HEAD)
    scores = jnp.einsum(
        "bgrd,bcgd->bgrc", query_heads, key_rows, preferred_element_type=jnp.float32
    ) * HEAD ** (-0.5)
    position = lax.axis_index("kvp") * ctx_dev + jnp.arange(ctx_dev, dtype=jnp.int32)
    valid_key = (position[None, :] < lengths[:, None])[:, None, None, :]
    masked = jnp.where(valid_key, scores, NEGATIVE)
    block_max = jnp.max(masked, axis=3)
    weights = jnp.where(valid_key, jnp.exp(masked - block_max[..., None]), 0.0)
    rounded = weights.astype(jnp.bfloat16)
    block_sum = jnp.sum(rounded.astype(jnp.float32), axis=3)
    block_out = jnp.einsum(
        "bgrc,bcgd->bgrd", rounded, value_rows, preferred_element_type=jnp.float32
    )
    global_max, denominator, summed = merged(
        (block_max, block_sum, block_out), "kvp", merge_partial
    )
    attended = (summed / denominator[..., None]).reshape(batch_size, local_heads * HEAD)
    projected = lax.psum(
        jnp.dot(attended.astype(jnp.bfloat16), out_weight, preferred_element_type=jnp.float32), "tp"
    )
    hidden_state = lax.optimization_barrier(
        (projected + residual.astype(jnp.float32)).astype(jnp.bfloat16)
    )
    state_wide = hidden_state.astype(jnp.float32)
    col_count = hidden_state.shape[1]
    exp_dev = w_gate.shape[0]
    experts = exp_dev * shards
    capacity = min(batch_size, max(2, 2 * batch_size * expert_ids.shape[1] // experts))
    dispatch, combine = slot_tables(expert_ids, gate_probs, experts, capacity)
    total_sq = lax.psum(jnp.sum(state_wide * state_wide, axis=1), "kvp")
    inverse = lax.rsqrt(total_sq / D + EPSILON)
    normed = (state_wide * inverse[:, None] * norm_gain.astype(jnp.float32)[None, :]).astype(
        jnp.bfloat16
    )
    outgoing = jnp.dot(
        dispatch.T.astype(jnp.bfloat16), normed, preferred_element_type=jnp.float32
    ).astype(jnp.bfloat16)
    outgoing = outgoing.reshape(experts, capacity, col_count)
    expert_rows = lax.all_to_all(outgoing, "kvp", split_axis=0, concat_axis=2, tiled=True)
    gate_proj = jnp.einsum("ecd,edf->ecf", expert_rows, w_gate, preferred_element_type=jnp.float32)
    up_proj = jnp.einsum("ecd,edf->ecf", expert_rows, w_up, preferred_element_type=jnp.float32)
    activation = (jax.nn.silu(gate_proj) * up_proj).astype(jnp.bfloat16)
    partial_value = jnp.einsum(
        "ecf,efd->ecd", activation, w_down, preferred_element_type=jnp.float32
    )
    returned = lax.all_to_all(partial_value, "kvp", split_axis=2, concat_axis=0, tiled=True)
    moe_local = jnp.dot(
        combine, returned.reshape(experts * capacity, col_count), precision=lax.Precision.HIGHEST
    )
    moe_term = lax.psum(moe_local, "tp")
    mixed = (state_wide + moe_term).astype(jnp.bfloat16)
    return (attended, mixed)


def solution(mesh):
    return jax.shard_map(
        on_device,
        mesh=mesh,
        in_specs=(
            P("grp", "tp"),
            P("grp", "kvp", "tp"),
            P("grp", "kvp", "tp"),
            P("grp"),
            P("tp", "kvp"),
            P("grp", "kvp"),
            P("kvp"),
            P("grp", None),
            P("grp", None),
            P("kvp", None, "tp"),
            P("kvp", None, "tp"),
            P("kvp", "tp", None),
        ),
        out_specs=(P("grp", "tp"), P("grp", "kvp")),
        check_vma=False,
    )
```

profile of v0, /device:TPU:0, one launch (start us, length us, event | category | flops | bytes accessed | tf_op | source)
XLA Modules:
  0.0 124.9 jit_solution(10427162739778779653)
XLA Ops:
  0.7 0.8 convert_element_type.54
  1.4 0.8 copy.99
  2.6 1.3 %multiply_add_fusion = s32[16,4]{0,1:T(4,128)} fusion(s32[16,4]{0,1:T(4,128)S(1)} %copy.100, s32[16,4]{0,1:T(4,128)} %param.21), kind=kLoop, calls=%fused_computation.48 | loop fusion | flops 128 | bytes 768 | tf_op jit(solution)/shard_map/add | solution.py:32
  3.9 0.9 reshape.104
  4.8 1.4 %copy.90 = bf16[16,128,128]{1,2,0:T(8,128)(2,1)S(1)} copy(bf16[16,128,128]{2,1,0:T(8,128)(2,1)} %param.15) | data formatting | bytes 1048576 | tf_op args[1]
  6.6 14.9 %all-gather = f32[64,2,8]{2,1,0:T(2,128)S(1)} all-gather(f32[16,2,8]{2,1,0:T(2,128)S(1)} %get-tuple-element.236), channel_id=2, replica_groups=mesh['grp'=2,'kvp'=4,'tp'=4] {'kvp'}, dimensions={0}, use_global_device_ids=true | all-gather | bytes 5120 | tf_op jit(solution)/shard_map/all_gather | solution.py:13
  21.7 13.3 %all-gather.1 = f32[64,2,8]{2,1,0:T(2,128)S(1)} all-gather(f32[16,2,8]{2,1,0:T(2,128)S(1)} %convert_reduce_fusion), channel_id=3, replica_groups=mesh['grp'=2,'kvp'=4,'tp'=4] {'kvp'}, dimensions={0}, use_global_device_ids=true | all-gather | bytes 5120 | tf_op jit(solution)/shard_map/all_gather | solution.py:13
  36.1 15.1 %all-gather.2 = f32[64,2,8,64]{3,2,1,0:T(8,128)S(1)} all-gather(f32[16,2,8,64]{3,2,1,0:T(8,128)S(1)} %fusion.35), channel_id=4, replica_groups=mesh['grp'=2,'kvp'=4,'tp'=4] {'kvp'}, dimensions={0}, use_global_device_ids=true | all-gather | bytes 327680 | tf_op jit(solution)/shard_map/all_gather | solution.py:13
  51.3 1.1 while.19
  52.6 0.7 reshape.107
  53.4 2.1 %fusion.18 = f32[16,384]{1,0:T(8,128)} fusion(bf16[1024,384]{1,0:T(8,128)(2,1)} %param.18, f32[16,1024]{1,0:T(8,128)} %reshape.107), kind=kOutput, calls=%fused_computation.30 | convolution fusion | flops 12599296 | bytes 876544 | tf_op jit(solution)/shard_map/dot_general | solution.py:93
  55.4 11.4 %psum.21 = f32[16,384]{1,0:T(8,128)} all-reduce(f32[16,384]{1,0:T(8,128)} %fusion.18), channel_id=1, replica_groups=mesh['grp'=2,'kvp'=4,'tp'=4] {'tp'}, use_global_device_ids=true, to_apply=%region_4.5 | all-reduce | flops 6144 | bytes 49152 | tf_op jit(solution)/shard_map/psum | solution.py:92
  66.8 0.7 add_convert_fusion
  68.2 12.5 %psum.22 = f32[16]{0:T(128)} all-reduce(f32[16]{0:T(128)} %fusion.21), channel_id=1, replica_groups=mesh['grp'=2,'kvp'=4,'tp'=4] {'kvp'}, use_global_device_ids=true, to_apply=%region_9.10 | all-reduce | flops 16 | bytes 128 | tf_op jit(solution)/shard_map/psum | solution.py:104
  80.7 0.7 add_rsqrt_fusion
  81.4 1.4 %convert_reduce_fusion.1 = (bf16[16,64]{1,0:T(8,128)(2,1)S(1)}, f32[16,64]{1,0:T(8,128)}) fusion(s32[16,4]{0,1:T(4,128)} %multiply_add_fusion, f32[16,4]{0,1:T(4,128)} %param.22), kind=kLoop, calls=%fused_computation.25 | loop fusion | flops 18432 | bytes 6656 | tf_op jit(solution)/shard_map/reduce_sum | solution.py:36
  82.9 8.1 %all_to_all.30 = bf16[4,16,384]{2,1,0:T(8,128)(2,1)S(1)} all-to-all(bf16[4,16,384]{2,1,0:T(8,128)(2,1)S(1)} %bitcast.73), channel_id=1, replica_groups=mesh['grp'=2,'kvp'=4,'tp'=4] {'kvp'}, dimensions={0} | all-to-all | bytes 98304 | tf_op jit(solution)/shard_map/all_to_all | solution.py:113
  91.6 1.7 %fusion.7 = f32[16,384]{1,0:T(8,128)} fusion(bf16[16,1536]{1,0:T(8,128)(2,1)} %bitcast.23, bf16[1,1536,384]{2,1,0:T(8,128)(2,1)S(1)} %copy-done.2), kind=kOutput, calls=%fused_computation.12 | convolution fusion | flops 18874368 | bytes 1253376 | tf_op jit(solution)/shard_map/ecd,edf->ecf/dot_general | solution.py:114
  93.3 1.6 %fusion.3 = f32[16,1536]{0,1:T(8,128)S(1)} fusion(bf16[1,384,1536]{2,1,0:T(8,128)(2,1)S(1)} %copy-done, bf16[16,1536]{1,0:T(8,128)(2,1)} %bitcast.23, bf16[1,1536,384]{2,1,0:T(8,128)(2,1)S(1)} %copy-done.1, f32[16,384]{1,0:T(8,128)} %fusion.7), kind=kOutput, calls=%fused_computation.8 | convolution fusion | flops 37785600 | bytes 2531328 | tf_op jit(solution)/shard_map/ecf,efd->ecd/dot_general | solution.py:117
  95.6 7.2 %reduce = f32[1536,16]{1,0:T(8,128)S(1)} reduce(f32[1536,1,16]{2,1,0:T(1,128)S(1)} %bitcast.66, f32[]{:T(128)} %broadcast.55), dimensions={1}, to_apply=%bitcast.47.reduce_sub_computation | reduce | bytes 196612
  103.1 8.2 %all_to_all.31 = f32[4,1,6144]{2,1,0:T(1,128)S(1)} all-to-all(f32[4,1,6144]{2,1,0:T(1,128)S(1)} %reshape.123), channel_id=1, replica_groups=mesh['grp'=2,'kvp'=4,'tp'=4] {'kvp'}, dimensions={0} | all-to-all | bytes 196608 | tf_op jit(solution)/shard_map/all_to_all | solution.py:120
  111.3 0.9 reduce.1
  112.3 1.3 %reshape.124 = f32[1536,1,16]{2,1,0:T(1,128)S(1)} reshape(f32[4,6144]{1,0:T(4,128)S(1)} %reduce.1) | data formatting | bytes 196608
  114.0 10.3 %psum.23 = f32[16,384]{1,0:T(8,128)S(1)} all-reduce(f32[16,384]{1,0:T(8,128)S(1)} %fusion.40), channel_id=1, replica_groups=mesh['grp'=2,'kvp'=4,'tp'=4] {'tp'}, use_global_device_ids=true, to_apply=%region_10.11 | all-reduce | flops 6144 | bytes 49152 | tf_op jit(solution)/shard_map/psum | solution.py:124
  (53 shorter events, 6.8 us)
Async XLA Ops:
  0.6 92.7 %copy-start = (bf16[1,384,1536]{2,1,0:T(8,128)(2,1)S(1)}, bf16[1,384,1536]{2,1,0:T(8,128)(2,1)}, u32[]{:S(2)}) copy-start(bf16[1,384,1536]{2,1,0:T(8,128)(2,1)} %param.25) | copy-start | bytes 3538948
  0.6 5.5 %copy-start.5 = (s32[16]{0:T(128)S(1)}, s32[16]{0:T(128)}, u32[]{:S(2)}) copy-start(s32[16]{0:T(128)} %param.17) | copy-start | bytes 196
  4.8 30.6 %copy-start.3 = (bf16[16,128,128]{2,1,0:T(8,128)(2,1)S(1)}, bf16[16,128,128]{2,1,0:T(8,128)(2,1)}, u32[]{:S(2)}) copy-start(bf16[16,128,128]{2,1,0:T(8,128)(2,1)} %param.16) | copy-start | bytes 1572868
  52.4 39.2 %copy-start.2 = (bf16[1,1536,384]{2,1,0:T(8,128)(2,1)S(1)}, bf16[1,1536,384]{2,1,0:T(8,128)(2,1)}, u32[]{:S(2)}) copy-start(bf16[1,1536,384]{2,1,0:T(8,128)(2,1)} %param.23) | copy-start | bytes 3538948
  53.4 40.0 %copy-start.1 = (bf16[1,1536,384]{2,1,0:T(8,128)(2,1)S(1)}, bf16[1,1536,384]{2,1,0:T(8,128)(2,1)}, u32[]{:S(2)}) copy-start(bf16[1,1536,384]{2,1,0:T(8,128)(2,1)} %param.24) | copy-start | bytes 3538948
  103.1 10.8 %copy-start.4 = (f32[16,64]{1,0:T(8,128)S(1)}, f32[16,64]{1,0:T(8,128)}, u32[]{:S(2)}) copy-start(f32[16,64]{1,0:T(8,128)} %get-tuple-element.217) | copy-start | bytes 12292
where the time goes:
time: 126 us; the launch traced here: 125 us
  blocking collectives  93.8 us (74%)
  other arithmetic  15.3 us (12%)
  local copies, waits for them, and re-layouts  8.31 us (7%)
  matrix products  6.53 us (5%)
    all_gather x3, blocking collectives, merged(): gathered = jax.tree.map(lambda a: lax.all_gather(a, axis), part)  43.4 us
    psum x1, blocking collectives, on_device(): total_sq = lax.psum(jnp.sum(state_wide * state_wide, axis=1), 'kvp')  12.5 us
    psum x1, blocking collectives, on_device(): lax.psum(jnp.dot(attended.astype(jnp.bfloat16), out_weight, preferred_ele...  11.4 us
    psum x1, blocking collectives, on_device(): moe_term = lax.psum(moe_local, 'tp')  10.3 us
    all_to_all x1, blocking collectives, on_device(): lax.all_to_all(partial_value, 'kvp', split_axis=2, concat_axis=0, tiled=T...  8.21 us
    all_to_all x1, blocking collectives, on_device(): lax.all_to_all(outgoing, 'kvp', split_axis=0, concat_axis=2, tiled=True)  8.06 us
    unnamed x1, other arithmetic  7.21 us
    unnamed x19, local copies, waits for them, and re-layouts  5.3 us

commit v1 on v0

--- a/solution.py
+++ b/solution.py
@@ -89,8 +89,12 @@
         (block_max, block_sum, block_out), "kvp", merge_partial
     )
     attended = (summed / denominator[..., None]).reshape(batch_size, local_heads * HEAD)
-    projected = lax.psum(
-        jnp.dot(attended.astype(jnp.bfloat16), out_weight, preferred_element_type=jnp.float32), "tp"
+    projected = jnp.sum(
+        lax.all_gather(
+            jnp.dot(attended.astype(jnp.bfloat16), out_weight, preferred_element_type=jnp.float32),
+            "tp",
+        ),
+        axis=0,
     )
     hidden_state = lax.optimization_barrier(
         (projected + residual.astype(jnp.float32)).astype(jnp.bfloat16)

time: 126 us -> 121 us (0.960)
  blocking collectives: 93.8 us -> 88.4 us
  other arithmetic: 15.3 us -> 16.9 us
    psum x1 -> x0, blocking collectives: 11.4 us -> none  [on_device(): lax.psum(jnp.dot(attended.astype(jnp.bfloat16), out_weight, preferred_ele...]
    all_gather x0 -> x1, blocking collectives: none -> 5.91 us  [on_device(): lax.all_gather(jnp.dot(attended.astype(jnp.bfloat16), out_weight, preferr...]
    reduce_sum x0 -> x1, other arithmetic: none -> 1.51 us  [on_device(): jnp.sum(lax.all_gather(jnp.dot(attended.astype(jnp.bfloat16), out_weight,...]
    unnamed x19 -> x21, local copies, waits for them, and re-layouts: 5.3 us -> 5.92 us
where the time goes in v1:
time: 121 us; the launch traced here: 120 us
  blocking collectives  88.4 us (73%)
  other arithmetic  16.9 us (14%)
  local copies, waits for them, and re-layouts  8.31 us (7%)
  matrix products  5.77 us (5%)
    all_gather x3, blocking collectives, merged(): gathered = jax.tree.map(lambda a: lax.all_gather(a, axis), part)  43.4 us
    psum x1, blocking collectives, on_device(): total_sq = lax.psum(jnp.sum(state_wide * state_wide, axis=1), 'kvp')  12.5 us
    psum x1, blocking collectives, on_device(): moe_term = lax.psum(moe_local, 'tp')  10.3 us
    all_to_all x1, blocking collectives, on_device(): lax.all_to_all(partial_value, 'kvp', split_axis=2, concat_axis=0, tiled=T...  8.21 us
    all_to_all x1, blocking collectives, on_device(): lax.all_to_all(outgoing, 'kvp', split_axis=0, concat_axis=2, tiled=True)  8.06 us
    unnamed x1, other arithmetic  7.21 us
    unnamed x21, local copies, waits for them, and re-layouts  5.92 us
    all_gather x1, blocking collectives, on_device(): lax.all_gather(jnp.dot(attended.astype(jnp.bfloat16), out_weight, preferr...  5.91 us

profile of v1, /device:TPU:0, one launch (start us, length us, event | category | flops | bytes accessed | tf_op | source)
XLA Modules:
  0.0 120.2 jit_solution(18288120567834153666)
XLA Ops:
  0.7 0.8 convert_element_type.54
  1.4 0.8 copy.99
  2.6 1.3 %multiply_add_fusion = s32[16,4]{0,1:T(4,128)} fusion(s32[16,4]{0,1:T(4,128)S(1)} %copy.100, s32[16,4]{0,1:T(4,128)} %param.21), kind=kLoop, calls=%fused_computation.48 | loop fusion | flops 128 | bytes 768 | tf_op jit(solution)/shard_map/add | solution.py:32
  3.9 0.9 reshape.104
  4.8 1.4 %copy.90 = bf16[16,128,128]{1,2,0:T(8,128)(2,1)S(1)} copy(bf16[16,128,128]{2,1,0:T(8,128)(2,1)} %param.15) | data formatting | bytes 1048576 | tf_op args[1]
  6.6 14.9 %all-gather = f32[64,2,8]{2,1,0:T(2,128)S(1)} all-gather(f32[16,2,8]{2,1,0:T(2,128)S(1)} %get-tuple-element.236), channel_id=2, replica_groups=mesh['grp'=2,'kvp'=4,'tp'=4] {'kvp'}, dimensions={0}, use_global_device_ids=true | all-gather | bytes 5120 | tf_op jit(solution)/shard_map/all_gather | solution.py:13
  21.8 13.3 %all-gather.1 = f32[64,2,8]{2,1,0:T(2,128)S(1)} all-gather(f32[16,2,8]{2,1,0:T(2,128)S(1)} %convert_reduce_fusion), channel_id=3, replica_groups=mesh['grp'=2,'kvp'=4,'tp'=4] {'kvp'}, dimensions={0}, use_global_device_ids=true | all-gather | bytes 5120 | tf_op jit(solution)/shard_map/all_gather | solution.py:13
  36.2 15.1 %all-gather.2 = f32[64,2,8,64]{3,2,1,0:T(8,128)S(1)} all-gather(f32[16,2,8,64]{3,2,1,0:T(8,128)S(1)} %fusion.35), channel_id=4, replica_groups=mesh['grp'=2,'kvp'=4,'tp'=4] {'kvp'}, dimensions={0}, use_global_device_ids=true | all-gather | bytes 327680 | tf_op jit(solution)/shard_map/all_gather | solution.py:13
  51.3 1.1 while.19
  53.4 1.3 %fusion.18 = f32[16,384]{1,0:T(8,128)S(1)} fusion(bf16[1024,384]{1,0:T(8,128)(2,1)} %param.18, f32[16,1024]{1,0:T(8,128)S(1)} %reshape.107), kind=kOutput, calls=%fused_computation.30 | convolution fusion | flops 12599296 | bytes 876544 | tf_op jit(solution)/shard_map/dot_general | solution.py:94
  54.7 5.9 %all-gather.3 = f32[64,384]{1,0:T(8,128)} all-gather(f32[16,384]{1,0:T(8,128)S(1)} %fusion.18), channel_id=5, replica_groups=mesh['grp'=2,'kvp'=4,'tp'=4] {'tp'}, dimensions={0}, use_global_device_ids=true | all-gather | bytes 122880 | tf_op jit(solution)/shard_map/all_gather | solution.py:93
  60.6 1.5 %reduce_sum.57 = f32[16,384]{1,0:T(8,128)} reduce(f32[4,16,384]{2,1,0:T(8,128)} %bitcast.72, f32[]{:T(128)} %constant.74.clone.1), dimensions={0}, to_apply=%region_4.5 | reduce | flops 18432 | bytes 122884 | tf_op jit(solution)/shard_map/reduce_sum | solution.py:92
  62.1 0.7 add_convert_fusion
  63.5 12.5 %psum.14 = f32[16]{0:T(128)} all-reduce(f32[16]{0:T(128)} %fusion.21), channel_id=1, replica_groups=mesh['grp'=2,'kvp'=4,'tp'=4] {'kvp'}, use_global_device_ids=true, to_apply=%region_9.10 | all-reduce | flops 16 | bytes 128 | tf_op jit(solution)/shard_map/psum | solution.py:108
  76.0 0.7 add_rsqrt_fusion
  76.7 1.4 %convert_reduce_fusion.1 = (bf16[16,64]{1,0:T(8,128)(2,1)S(1)}, f32[16,64]{1,0:T(8,128)}) fusion(s32[16,4]{0,1:T(4,128)} %multiply_add_fusion, f32[16,4]{0,1:T(4,128)} %param.22), kind=kLoop, calls=%fused_computation.25 | loop fusion | flops 18432 | bytes 6656 | tf_op jit(solution)/shard_map/reduce_sum | solution.py:36
  78.3 8.1 %all_to_all.30 = bf16[4,16,384]{2,1,0:T(8,128)(2,1)S(1)} all-to-all(bf16[4,16,384]{2,1,0:T(8,128)(2,1)S(1)} %bitcast.75), channel_id=1, replica_groups=mesh['grp'=2,'kvp'=4,'tp'=4] {'kvp'}, dimensions={0} | all-to-all | bytes 98304 | tf_op jit(solution)/shard_map/all_to_all | solution.py:117
  87.0 1.7 %fusion.7 = f32[16,384]{1,0:T(8,128)} fusion(bf16[16,1536]{1,0:T(8,128)(2,1)} %bitcast.24, bf16[1,1536,384]{2,1,0:T(8,128)(2,1)S(1)} %copy-done.2), kind=kOutput, calls=%fused_computation.12 | convolution fusion | flops 18874368 | bytes 1253376 | tf_op jit(solution)/shard_map/ecd,edf->ecf/dot_general | solution.py:118
  88.7 1.6 %fusion.3 = f32[16,1536]{0,1:T(8,128)S(1)} fusion(bf16[1,384,1536]{2,1,0:T(8,128)(2,1)S(1)} %copy-done, bf16[16,1536]{1,0:T(8,128)(2,1)} %bitcast.24, bf16[1,1536,384]{2,1,0:T(8,128)(2,1)S(1)} %copy-done.1, f32[16,384]{1,0:T(8,128)} %fusion.7), kind=kOutput, calls=%fused_computation.8 | convolution fusion | flops 37785600 | bytes 2531328 | tf_op jit(solution)/shard_map/ecf,efd->ecd/dot_general | solution.py:121
  90.9 7.2 %reduce = f32[1536,16]{1,0:T(8,128)S(1)} reduce(f32[1536,1,16]{2,1,0:T(1,128)S(1)} %bitcast.67, f32[]{:T(128)} %broadcast.55), dimensions={1}, to_apply=%bitcast.48.reduce_sub_computation | reduce | bytes 196612
  98.4 8.2 %all_to_all.31 = f32[4,1,6144]{2,1,0:T(1,128)S(1)} all-to-all(f32[4,1,6144]{2,1,0:T(1,128)S(1)} %reshape.124), channel_id=1, replica_groups=mesh['grp'=2,'kvp'=4,'tp'=4] {'kvp'}, dimensions={0} | all-to-all | bytes 196608 | tf_op jit(solution)/shard_map/all_to_all | solution.py:124
  106.7 0.9 reduce.1
  107.6 1.3 %reshape.125 = f32[1536,1,16]{2,1,0:T(1,128)S(1)} reshape(f32[4,6144]{1,0:T(4,128)S(1)} %reduce.1) | data formatting | bytes 196608
  109.4 10.3 %psum.15 = f32[16,384]{1,0:T(8,128)S(1)} all-reduce(f32[16,384]{1,0:T(8,128)S(1)} %fusion.40), channel_id=1, replica_groups=mesh['grp'=2,'kvp'=4,'tp'=4] {'tp'}, use_global_device_ids=true, to_apply=%region_10.11 | all-reduce | flops 6144 | bytes 49152 | tf_op jit(solution)/shard_map/psum | solution.py:128
  (56 shorter events, 7.5 us)
Async XLA Ops:
  0.6 88.1 %copy-start = (bf16[1,384,1536]{2,1,0:T(8,128)(2,1)S(1)}, bf16[1,384,1536]{2,1,0:T(8,128)(2,1)}, u32[]{:S(2)}) copy-start(bf16[1,384,1536]{2,1,0:T(8,128)(2,1)} %param.25) | copy-start | bytes 3538948
  0.6 5.6 %copy-start.6 = (s32[16]{0:T(128)S(1)}, s32[16]{0:T(128)}, u32[]{:S(2)}) copy-start(s32[16]{0:T(128)} %param.17) | copy-start | bytes 196
  4.8 30.6 %copy-start.3 = (bf16[16,128,128]{2,1,0:T(8,128)(2,1)S(1)}, bf16[16,128,128]{2,1,0:T(8,128)(2,1)}, u32[]{:S(2)}) copy-start(bf16[16,128,128]{2,1,0:T(8,128)(2,1)} %param.16) | copy-start | bytes 1572868
  52.5 34.5 %copy-start.2 = (bf16[1,1536,384]{2,1,0:T(8,128)(2,1)S(1)}, bf16[1,1536,384]{2,1,0:T(8,128)(2,1)}, u32[]{:S(2)}) copy-start(bf16[1,1536,384]{2,1,0:T(8,128)(2,1)} %param.23) | copy-start | bytes 3538948
  52.8 0.6 copy-start.4
  54.7 34.0 %copy-start.1 = (bf16[1,1536,384]{2,1,0:T(8,128)(2,1)S(1)}, bf16[1,1536,384]{2,1,0:T(8,128)(2,1)}, u32[]{:S(2)}) copy-start(bf16[1,1536,384]{2,1,0:T(8,128)(2,1)} %param.24) | copy-start | bytes 3538948
  98.4 10.8 %copy-start.5 = (f32[16,64]{1,0:T(8,128)S(1)}, f32[16,64]{1,0:T(8,128)}, u32[]{:S(2)}) copy-start(f32[16,64]{1,0:T(8,128)} %get-tuple-element.217) | copy-start | bytes 12292
